TPU v7x, 128 devices: a whole 4x4x4 slice. The times are simulated.
128 devices in a mesh: seq: 16 (over x, z), head: 8 (over y, core).
Axes of the slice: x: 4, y: 4, z: 4, core: 2. Of those that a mesh axis runs over, the one named last changes fastest.
Arguments:
- context: bfloat16 [8, 8192, 1024], P('head', 'seq'), may hold values from -6 to 6
- latents: bfloat16 [8, 1024, 1024], P('head'), may hold values from -6 to 6
- offsets: int32 [8], P('head'), may hold values from 0 to 7168
- query_gain: float32 [1024], replicated, may hold values from 0.1 to 1.9
- key_gain: float32 [1024], replicated, may hold values from 0.1 to 1.9
- layer_gain: float32 [2, 1024], replicated, may hold values from 0.1 to 1.9
- cross_query: bfloat16 [1024, 1024], P(('seq', 'head')), may hold values from -0.25 to 0.25
- cross_key: bfloat16 [1024, 1024], P(('seq', 'head')), may hold values from -0.25 to 0.25
- cross_value: bfloat16 [1024, 1024], P(('seq', 'head')), may hold values from -0.1875 to 0.1875
- cross_out: bfloat16 [1024, 1024], P(('seq', 'head')), may hold values from -0.1875 to 0.1875
- layer_qkv: bfloat16 [2, 1024, 3072], P(None, ('seq', 'head')), may hold values from -0.25 to 0.25
- layer_out: bfloat16 [2, 1024, 1024], P(None, ('seq', 'head')), may hold values from -0.1875 to 0.1875
Outputs:
- latent_out: bfloat16 [8, 1024, 1024], P('head', 'seq')
Inputs may be any that keep to these rules, and one draw needn't show every extreme that they name: Latent i of row b stands at context position offsets[b] + i.
All inputs are finite; a program needn't handle non-finite values.
Results may differ from a plain program's by a relative error of at most 0.013.
Values may be sent and summed in bfloat16 or wider, within the bound.
A program may use at most 128 MiB of HBM per device.

v0:
```python
import functools

import jax
import jax.numpy as jnp
from jax import lax
from jax.experimental import pallas as pl
from jax.experimental.pallas import tpu as pltpu
from jax.sharding import PartitionSpec as P

H = 16
EPSILON = 1e-06
NEGATIVE = -1e30
BF = jnp.bfloat16
F32 = jnp.float32
MESH = pl.DeviceIdType.MESH
N = 16
D = 1024


def normed_rows(x, gain):
    x = x.astype(F32)
    scale = lax.rsqrt(jnp.mean(x * x, axis=-1, keepdims=True) + EPSILON)
    return (x * scale * gain).astype(BF)


def dot(a, b):
    return jnp.dot(a, b, preferred_element_type=F32)


def dot_t(a, b):
    return lax.dot_general(a, b, (((1,), (1,)), ((), ())), preferred_element_type=F32)


def lanes(rows, width=128):
    return lax.broadcasted_iota(jnp.int32, (rows, width), 1)


def greet(me):
    barrier = pltpu.get_barrier_semaphore()

    @pl.loop(1, N)
    def _(d):
        pl.semaphore_signal(
            barrier, inc=1, device_id={"seq": lax.rem(me + d, N)}, device_id_type=MESH
        )


def greeted():
    pl.semaphore_wait(pltpu.get_barrier_semaphore(), N - 1)


def push(me, d, src, dst, send_sem, recv_sem):
    return pltpu.make_async_remote_copy(
        src_ref=src,
        dst_ref=dst,
        send_sem=send_sem,
        recv_sem=recv_sem,
        device_id={"seq": lax.rem(me + d, N)},
        device_id_type=MESH,
    )


def cross_kernel(
    off_ref, ctx_any, lat_any, qg_ref, kg_ref, w_any, out_ref,
    ctx, lat, w, cn, ln, keys, vals, queries, bias, part, stat, got, gstat, acc, den,
    load_sem, send_sem, recv_sem, ssend_sem, srecv_sem,
):
    me = lax.axis_index("seq")
    greet(me)
    loads = [
        pltpu.make_async_copy(ctx_any, ctx, load_sem.at[0]),
        pltpu.make_async_copy(w_any.at[:, pl.ds(D, 2 * D)], w.at[:, pl.ds(D, 2 * D)], load_sem.at[1]),
        pltpu.make_async_copy(lat_any, lat, load_sem.at[2]),
        pltpu.make_async_copy(w_any.at[:, pl.ds(0, D)], w.at[:, pl.ds(0, D)], load_sem.at[3]),
    ]
    for c in loads:
        c.start()
    C = ctx.shape[0]
    M = lat.shape[0]
    R = M // N
    S = 128
    edge = me * C - off_ref[0]
    loads[0].wait()

    @pl.loop(0, C // S)
    def _(r):
        rows = pl.ds(pl.multiple_of(r * S, S), S)
        cn[rows] = normed_rows(ctx[rows], kg_ref[...])

    loads[2].wait()

    @pl.loop(0, M // S)
    def _(r):
        rows = pl.ds(pl.multiple_of(r * S, S), S)
        ln[rows] = normed_rows(lat[rows], qg_ref[...])
        i = lax.broadcasted_iota(jnp.int32, (S, C), 0) + r * S
        j = lax.broadcasted_iota(jnp.int32, (S, C), 1)
        bias[rows] = jnp.where(j + edge <= i, 0.0, NEGATIVE)

    stat[...] = jnp.zeros_like(stat)
    loads[1].wait()

    @pl.loop(0, D // 256)
    def _(n):
        kc = pl.ds(pl.multiple_of(D + n * 256, 256), 256)
        vc = pl.ds(pl.multiple_of(2 * D + n * 256, 256), 256)
        k = dot(cn[...], w[:, kc]).astype(BF)
        keys[2 * n] = k[:, :128]
        keys[2 * n + 1] = k[:, 128:]
        v = dot(cn[...], w[:, vc]).astype(BF)
        for t in range(2):
            vals[2 * n + t, :, 0:128] = v[:, 128 * t : 128 * t + 128]
            vals[2 * n + t, :, 128:256] = jnp.ones((C, 128), BF)

    loads[3].wait()

    @pl.loop(0, D // 256)
    def _(n):
        qc = pl.ds(pl.multiple_of(n * 256, 256), 256)

        @pl.loop(0, 2)
        def _(m):
            rows = pl.ds(pl.multiple_of(m * (M // 2), M // 2), M // 2)
            q = dot(ln[rows], w[:, qc]).astype(BF) * 0.125
            queries[2 * n, rows] = q[:, :128]
            queries[2 * n + 1, rows] = q[:, 128:]

    greeted()
    T = 128

    @pl.loop(0, H // 2)
    def _(p):
        @pl.loop(0, M // T)
        def _(r):
            rows = pl.ds(pl.multiple_of(r * T, T), T)
            q = queries[p, rows]
            low = lanes(T) < 64
            outs = []
            st = stat[rows]
            for t in range(2):
                qt = jnp.where(low if t == 0 else ~low, q, jnp.zeros_like(q))
                s = dot_t(qt, keys[p]) + bias[rows]
                top = jnp.max(s, axis=1, keepdims=True)
                e = jnp.exp(s - top).astype(BF)
                o = dot(e, vals[p])
                total = o[:, 128:256]
                outs.append(o[:, 0:128] / total)
                st = jnp.where(lanes(T) == 2 * p + t, top + jnp.log(total), st)
            part[p, rows] = jnp.where(low, outs[0], outs[1]).astype(BF)
            stat[rows] = st

        @pl.loop(1, N)
        def _(d):
            there = pl.ds(pl.multiple_of(lax.rem(me + d, N) * R, R), R)
            push(me, d, part.at[p, there], got.at[d - 1, p], send_sem, recv_sem.at[d - 1]).start()

    @pl.loop(1, N)
    def _(d):
        there = pl.ds(pl.multiple_of(lax.rem(me + d, N) * R, R), R)
        push(me, d, stat.at[there], gstat.at[d - 1], ssend_sem, srecv_sem).start()

    own = pl.ds(pl.multiple_of(me * R, R), R)
    push(me, 1, gstat, gstat, ssend_sem, srecv_sem).wait_recv()
    top = stat[own]
    for d in range(N - 1):
        top = jnp.maximum(top, gstat[d])
    spread = (
        lax.broadcasted_iota(jnp.int32, (128, D), 1) // 64
        == lax.broadcasted_iota(jnp.int32, (128, D), 0)
    ).astype(F32).astype(BF)
    weight = dot(jnp.exp(stat[own] - top).astype(BF), spread)
    den[...] = weight
    for p in range(H // 2):
        cols = slice(128 * p, 128 * p + 128)
        acc[:, cols] = weight[:, cols] * part[p, own].astype(F32)

    @pl.loop(0, N - 1)
    def _(d):
        push(me, 1, got.at[d], got.at[d], send_sem, recv_sem.at[d]).wait_recv()
        weight = dot(jnp.exp(gstat[d] - top).astype(BF), spread)
        den[...] += weight
        for p in range(H // 2):
            cols = slice(128 * p, 128 * p + 128)
            acc[:, cols] += weight[:, cols] * got[d, p].astype(F32)

    out_ref[...] = (acc[...] / den[...]).astype(BF)
    push(me, 1, got, got, send_sem, recv_sem.at[0]).wait_send()
    push(me, 1, gstat, gstat, ssend_sem, srecv_sem).wait_send()


def layer_kernel(
    first, x_ref, y_ref, g_ref, w_any, out_ref,
    w, qkv, qk_out, v_out, qk_in, v_in, m_out, m_in, hid, merged,
    load_sem, send_sem, recv_sem,
):
    me = lax.axis_index("seq")
    greet(me)
    R = x_ref.shape[0]
    M = R * N
    base = D if first else 0
    loads = []
    cuts = ([(0, D)] if first else []) + [(base, 3 * D), (base + 3 * D, D)]
    for k, (start, size) in enumerate(cuts):
        cols = pl.ds(start, size)
        loads.append(pltpu.make_async_copy(w_any.at[:, cols], w.at[:, cols], load_sem.at[k]))
        loads[-1].start()
    if first:
        loads[0].wait()
        hidden = x_ref[...].astype(F32) + dot(y_ref[...], w[:, 0:D])
        hidden = hidden.astype(BF)
    else:
        hidden = x_ref[...]
    hid[...] = hidden
    normed = normed_rows(hidden, g_ref[...])
    loads[-2].wait()
    low = lanes(R) < 64
    half = R // 2

    def roll(a):
        return pltpu.roll(a.astype(F32), 64, 1).astype(BF)

    @pl.loop(0, 3 * D // 512)
    def _(n):
        cols = pl.ds(pl.multiple_of(n * 512, 512), 512)
        wide = pl.ds(pl.multiple_of(base + n * 512, 512), 512)
        qkv[:, cols] = dot(normed, w[:, wide]).astype(BF)

    lo = lanes(half) < 64
    for p in range(H // 2):
        q = qkv[:, 128 * p : 128 * p + 128] * 0.125
        k = qkv[:, D + 128 * p : D + 128 * p + 128]
        v = qkv[:, 2 * D + 128 * p : 2 * D + 128 * p + 128]
        qk_out[2 * p] = jnp.where(low, q, roll(k))
        qk_out[2 * p + 1] = jnp.where(low, roll(q), k)
        vr = roll(v)
        v_out[2 * p] = jnp.where(lo, v[:half], vr[half:])
        v_out[2 * p + 1] = jnp.where(lo, vr[:half], v[half:])
    greeted()

    @pl.loop(1, N)
    def _(d):
        to = lax.rem(me + d, N)
        push(me, d, qk_out.at[to], qk_in.at[me], send_sem.at[0], recv_sem.at[0]).start()
        push(me, d, v_out.at[to], v_in.at[me], send_sem.at[1], recv_sem.at[1]).start()

    qk_in[me] = qk_out[me]
    v_in[me] = v_out[me]
    rest = pl.ds(0, N - 1)
    push(me, 1, qk_in.at[rest], qk_in.at[rest], send_sem.at[0], recv_sem.at[0]).wait_recv()
    push(me, 1, v_in.at[rest], v_in.at[rest], send_sem.at[1], recv_sem.at[1]).wait_recv()

    qk = qk_in[...].reshape(M, 128)
    low_m = lanes(M) < 64
    kk = roll(qk)
    vp = v_in[...]
    vr = roll(vp.reshape(M // 2, 128)).reshape(N, half, 128)
    both = jnp.concatenate([vp, vr], axis=1).reshape(M, 128)
    vv = jnp.where(low_m, both, jnp.ones_like(both))
    T = 128
    for r in range(M // T):
        size = (r + 1) * T
        q = qk[r * T : size]
        q = jnp.where(lanes(T) < 64, q, jnp.zeros_like(q))
        s = dot_t(q, kk[:size])
        i = lax.broadcasted_iota(jnp.int32, (T, size), 0) + r * T
        j = lax.broadcasted_iota(jnp.int32, (T, size), 1)
        s = jnp.where(j <= i, s, NEGATIVE)
        top = jnp.max(s, axis=1, keepdims=True)
        e = jnp.exp(s - top).astype(BF)
        o = dot(e, vv[:size])
        mixed = o / pltpu.roll(o, 64, 1)
        other = pltpu.roll(mixed, 64, 1)
        for t in range(T // R):
            m_out[r * (T // R) + t] = jnp.where(
                lo, mixed[t * R : t * R + half], other[t * R + half : t * R + R]
            ).astype(BF)

    @pl.loop(1, N)
    def _(d):
        to = lax.rem(me + d, N)
        push(me, d, m_out.at[to], m_in.at[me], send_sem.at[2], recv_sem.at[2]).start()

    m_in[me] = m_out[me]
    push(me, 1, m_in.at[rest], m_in.at[rest], send_sem.at[2], recv_sem.at[2]).wait_recv()
    for p in range(H // 2):
        a = m_in[2 * p]
        b = m_in[2 * p + 1]
        merged[0:half, 128 * p : 128 * p + 128] = jnp.where(lo, a, roll(b))
        merged[half:R, 128 * p : 128 * p + 128] = jnp.where(lo, roll(a), b)
    loads[-1].wait()
    update = dot(merged[...], w[:, base + 3 * D : base + 4 * D])
    out_ref[...] = (hid[...].astype(F32) + update).astype(BF)
    push(me, 1, qk_in.at[rest], qk_in.at[rest], send_sem.at[0], recv_sem.at[0]).wait_send()
    push(me, 1, v_in.at[rest], v_in.at[rest], send_sem.at[1], recv_sem.at[1]).wait_send()
    push(me, 1, m_in.at[rest], m_in.at[rest], send_sem.at[2], recv_sem.at[2]).wait_send()


VM = pl.BlockSpec(memory_space=pltpu.VMEM)
SM = pl.BlockSpec(memory_space=pltpu.SMEM)
ANY = pl.BlockSpec(memory_space=pl.ANY)
DMA = pltpu.SemaphoreType.DMA


def params(which):
    return pltpu.CompilerParams(
        collective_id=which, has_side_effects=True, vmem_limit_bytes=48 << 20
    )


def cross(context, latents, offsets, query_gain, key_gain, weights):
    C, M = context.shape[0], latents.shape[0]
    R = M // N
    return pl.pallas_call(
        cross_kernel,
        out_shape=jax.ShapeDtypeStruct((R, D), BF),
        in_specs=[SM, ANY, ANY, VM, VM, ANY],
        out_specs=VM,
        scratch_shapes=[
            pltpu.VMEM((C, D), BF),
            pltpu.VMEM((M, D), BF),
            pltpu.VMEM((D, 3 * D), BF),
            pltpu.VMEM((C, D), BF),
            pltpu.VMEM((M, D), BF),
            pltpu.VMEM((H // 2, C, 128), BF),
            pltpu.VMEM((H // 2, C, 256), BF),
            pltpu.VMEM((H // 2, M, 128), BF),
            pltpu.VMEM((M, C), F32),
            pltpu.VMEM((H // 2, M, 128), BF),
            pltpu.VMEM((M, 128), F32),
            pltpu.VMEM((N - 1, H // 2, R, 128), BF),
            pltpu.VMEM((N - 1, R, 128), F32),
            pltpu.VMEM((R, D), F32),
            pltpu.VMEM((R, D), F32),
            DMA((4,)),
            DMA,
            DMA((N - 1,)),
            DMA,
            DMA,
        ],
        compiler_params=params(0),
        cost_estimate=pl.CostEstimate(
            flops=30 * 10**9, bytes_accessed=10 << 20, transcendentals=8 << 20
        ),
        name="cross",
    )(offsets, context, latents, query_gain, key_gain, weights)


def layer(which, hidden, attended, gain, weights):
    R = hidden.shape[0]
    first = which == 1
    return pl.pallas_call(
        functools.partial(layer_kernel, first),
        out_shape=jax.ShapeDtypeStruct((R, D), BF),
        in_specs=[VM, VM, VM, ANY],
        out_specs=VM,
        scratch_shapes=[
            pltpu.VMEM(weights.shape, BF),
            pltpu.VMEM((R, 3 * D), BF),
            pltpu.VMEM((H, R, 128), BF),
            pltpu.VMEM((H, R // 2, 128), BF),
            pltpu.VMEM((N, R, 128), BF),
            pltpu.VMEM((N, R // 2, 128), BF),
            pltpu.VMEM((N, R // 2, 128), BF),
            pltpu.VMEM((H, R // 2, 128), BF),
            pltpu.VMEM((R, D), BF),
            pltpu.VMEM((R, D), BF),
            DMA((3,)),
            DMA((3,)),
            DMA((3,)),
        ],
        compiler_params=params(which),
        cost_estimate=pl.CostEstimate(
            flops=10 * 10**9, bytes_accessed=10 << 20, transcendentals=1 << 20
        ),
        name=f"layer{which}",
    )(hidden, attended, gain, weights)


def per_device(
    context,
    latents,
    offsets,
    query_gain,
    key_gain,
    layer_gain,
    cross_query,
    cross_key,
    cross_value,
    cross_out,
    layer_qkv,
    layer_out,
):
    def gather(*pieces):
        return lax.all_gather(
            jnp.concatenate(pieces, axis=1), ("seq", "head"), axis=0, tiled=True
        )

    M = latents.shape[1]
    R = M // N
    w0 = gather(cross_query, cross_key, cross_value)
    w1 = gather(cross_out, layer_qkv[0], layer_out[0])
    w2 = gather(layer_qkv[1], layer_out[1])
    own = lax.dynamic_slice_in_dim(latents[0], lax.axis_index("seq") * R, R, 0)
    attended = cross(
        context[0], latents[0], offsets, query_gain[None], key_gain[None], w0
    )
    hidden = layer(1, own, attended, layer_gain[0:1], w1)
    hidden = layer(2, hidden, hidden, layer_gain[1:2], w2)
    return hidden[None]


def solution(mesh):
    return jax.shard_map(
        per_device,
        mesh=mesh,
        in_specs=(
            P("head", "seq", None),
            P("head", None, None),
            P("head"),
            P(),
            P(),
            P(),
            P(("seq", "head"), None),
            P(("seq", "head"), None),
            P(("seq", "head"), None),
            P(("seq", "head"), None),
            P(None, ("seq", "head"), None),
            P(None, ("seq", "head"), None),
        ),
        out_specs=P("head", "seq", None),
        check_vma=False,
    )
```

profile of v0, /device:TPU:0, one launch (start us, length us, event | category | flops | bytes accessed | tf_op | source)
XLA Modules:
  0.0 260.3 jit_solution(6704886944165208755)
XLA Ops:
  6.5 0.0 all-gather.4.cloned.1.call-start
  6.5 1.4 pad_maximum_fusion.2
  7.9 0.0 all-gather.4.cloned.1.call-update
  7.9 0.0 all-gather.6.cloned.1.call-start
  8.0 0.7 slice_bitcast_fusion.2
  8.7 0.8 slice_bitcast_fusion
  9.5 1.4 pad_maximum_fusion
  10.9 0.0 all-gather.6.cloned.1.call-update
  10.9 0.0 all-gather.8.cloned.1.call-start
  11.0 0.6 pad_maximum_fusion.1
  11.6 0.1 all-gather.8.cloned.1.call-update
  12.3 0.9 dynamic-slice_bitcast_fusion.x_ref
  13.2 0.8 fusion
  14.0 67.1 %all-gather.4.cloned.1.call-done.w_any = bf16[1024,3072]{1,0:T(8,128)(2,1)} async-done(((bf16[8,3072]{1,0:T(8,128)(2,1)}), bf16[1024,3072]{1,0:T(8,128)(2,1)}) %all-gather.4.cloned.1.call-update) | async-done | bytes 6291472 | tf_op jit(solution)/shard_map/all_gather | solution.py:394
  81.2 0.0 copy-start
  81.2 1.6 copy-done
  82.8 0.0 copy-start.1
  82.8 1.2 copy-done.1
  84.0 0.0 copy-start.2
  84.0 0.7 copy-done.2
  84.7 0.0 copy-start.3
  84.7 0.7 copy-done.3
  85.4 58.4 %cross.1.y_ref = bf16[64,1024]{1,0:T(8,128)(2,1)S(1)} custom-call(s32[1]{0:T(128)S(6)} %copy.14.off_ref, bf16[512,1024]{1,0:T(8,128)(2,1)S(1)} %bitcast.17, bf16[1024,1024]{1,0:T(8,128)(2,1)S(1)} %bitcast.16, f32[1,1024]{1,0:T(1,128)S(1)} %bitcast.18, f32[1,1024]{1,0:T(1,128)S(1)} %bitcast.19, bf16[1024,3072]{1,0:T(8,128)(2,1)} %all-gather.4.cloned.1.call-done.w_any), custom_call_target="tpu_custom_call" | custom-call | flops 30000001024 | bytes 10485760 | tf_op jit(solution)/shard_map/cross/pallas_call | solution.py:313
  143.8 16.7 %all-gather.6.cloned.1.call-done.w_any = bf16[1024,5120]{1,0:T(8,128)(2,1)} async-done(((bf16[8,5120]{1,0:T(8,128)(2,1)}), bf16[1024,5120]{1,0:T(8,128)(2,1)}) %all-gather.6.cloned.1.call-update) | async-done | bytes 10485776 | tf_op jit(solution)/shard_map/all_gather | solution.py:394
  160.5 22.7 %layer1.1.x_ref.y_ref = bf16[64,1024]{1,0:T(8,128)(2,1)S(1)} custom-call(bf16[64,1024]{1,0:T(8,128)(2,1)S(1)} %dynamic-slice_bitcast_fusion.x_ref, bf16[64,1024]{1,0:T(8,128)(2,1)S(1)} %cross.1.y_ref, f32[1,1024]{1,0:T(1,128)S(1)} %get-tuple-element.10.g_ref, bf16[1024,5120]{1,0:T(8,128)(2,1)} %all-gather.6.cloned.1.call-done.w_any), custom_call_target="tpu_custom_call" | custom-call | flops 10000000000 | bytes 10485760 | tf_op jit(solution)/shard_map/layer1/pallas_call | solution.py:351
  183.2 48.1 %all-gather.8.cloned.1.call-done.w_any = bf16[1024,4096]{1,0:T(8,128)(2,1)} async-done(((bf16[8,4096]{1,0:T(8,128)(2,1)}), bf16[1024,4096]{1,0:T(8,128)(2,1)}) %all-gather.8.cloned.1.call-update) | async-done | bytes 8388624 | tf_op jit(solution)/shard_map/all_gather | solution.py:394
  231.3 21.8 %layer2.1 = bf16[64,1024]{1,0:T(8,128)(2,1)S(1)} custom-call(bf16[64,1024]{1,0:T(8,128)(2,1)S(1)} %layer1.1.x_ref.y_ref, bf16[64,1024]{1,0:T(8,128)(2,1)S(1)} %layer1.1.x_ref.y_ref, f32[1,1024]{1,0:T(1,128)S(1)} %get-tuple-element.9.g_ref, bf16[1024,4096]{1,0:T(8,128)(2,1)} %all-gather.8.cloned.1.call-done.w_any), custom_call_target="tpu_custom_call" | custom-call | flops 10000000000 | bytes 10485760 | tf_op jit(solution)/shard_map/layer2/pallas_call | solution.py:351
  253.1 0.7 copy.15
Async XLA Ops:
  6.5 74.6 %all-gather.4.cloned.1.call-start = ((), (), s32[]{:S(2)}) async-start(), calls=%async_computation | async-start | bytes 6340608 | tf_op jit(solution)/shard_map/all_gather | solution.py:394
  7.9 152.6 %all-gather.6.cloned.1.call-start = ((), (), s32[]{:S(2)}) async-start(), calls=%async_computation.1 | async-start | bytes 10567680 | tf_op jit(solution)/shard_map/all_gather | solution.py:394
  10.9 220.4 %all-gather.8.cloned.1.call-start = ((), (), s32[]{:S(2)}) async-start(), calls=%async_computation.2 | async-start | bytes 8454144 | tf_op jit(solution)/shard_map/all_gather | solution.py:394
  81.2 1.6 copy-start
  82.8 1.2 copy-start.1
  84.0 0.7 copy-start.2
  84.7 0.7 copy-start.3
Sparse Core Ops, SparseCore 0:
  10.4 70.6 all-gather.3
  84.3 76.1 all-gather.5
  163.5 67.7 all-gather.7
where the time goes:
time: 261 us; the launch traced here: 260 us
  waiting for transfers between devices  132 us (51%)
  Pallas kernels  103 us (39%)
  between operations  13.8 us (5%)
  local copies, waits for them, and re-layouts  8.12 us (3%)
  other arithmetic  3.34 us (1%)
    all_gather x3, waiting for transfers between devices, gather(): lax.all_gather(jnp.concatenate(pieces, axis=1), ('seq', 'head'), axis=0,...  132 us
    pallas_call x1, Pallas kernels, cross(): pl.pallas_call(cross_kernel, out_shape=jax.ShapeDtypeStruct((R, D), BF),...  58.4 us
    pallas_call x2, Pallas kernels, layer(): pl.pallas_call(functools.partial(layer_kernel, first), out_shape=jax.Shap...  44.5 us
  transfers between devices with their start and end apart: 3, of which 3 were waited for; matrix products, arithmetic and copies ran while one was open for 2% of the time, Pallas kernels for 31%

commit v1 on v0

v1 whole, which is shorter than its diff:
```python
import functools

import jax
import jax.numpy as jnp
from jax import lax
from jax.experimental import pallas as pl
from jax.experimental.pallas import tpu as pltpu
from jax.sharding import PartitionSpec as P

H = 16
EPSILON = 1e-06
NEGATIVE = -1e30
BF = jnp.bfloat16
F32 = jnp.float32
MESH = pl.DeviceIdType.MESH
N = 16
D = 1024


def normed_rows(x, gain):
    x = x.astype(F32)
    scale = lax.rsqrt(jnp.mean(x * x, axis=-1, keepdims=True) + EPSILON)
    return (x * scale * gain).astype(BF)


def dot(a, b):
    return jnp.dot(a, b, preferred_element_type=F32)


def dot_t(a, b):
    return lax.dot_general(a, b, (((1,), (1,)), ((), ())), preferred_element_type=F32)


def lanes(rows, width=128):
    return lax.broadcasted_iota(jnp.int32, (rows, width), 1)


K = 4
ROUNDS = ((0, 1), (3, 2), (9, 1))


class Gather:
    def __init__(self, w, blank, sems):
        self.w, self.blank = w, blank
        self.near_sem, self.side_sem, self.far_sem, self.mate_sem, self.sent_sem = sems
        me, lane = lax.axis_index("seq"), lax.axis_index("head")
        self.me = me
        self.at = (me // K, lax.rem(me, K), lane // 2)
        self.core = lax.rem(lane, 2)

    def device(self, at, core=None):
        core = self.core if core is None else core
        return {"seq": at[0] * K + at[1], "head": at[2] * 2 + core}

    def plane(self, axis):
        a, b = [i for i in range(3) if i != axis]
        flat = self.at[a] * K + self.at[b]

        def peer(i):
            j = lax.rem(flat + i, K * K)
            at = list(self.at)
            at[a], at[b] = j // K, lax.rem(j, K)
            return at

        return peer

    def along(self, axis, step):
        at = list(self.at)
        at[axis] = lax.rem(at[axis] + step, K)
        return at

    def units(self, g, axis):
        start, k = ROUNDS[g]
        return pl.ds(start + axis * k, k)

    def own(self, g, axis):
        return self.w.at[(self.units(g, axis), *self.at, self.core)]

    def slab(self, g, axis, step, half=None):
        index = [slice(None)] * 3
        index[axis] = lax.rem(self.at[axis] + step, K)
        if half is not None:
            index[1 if axis == 0 else 0] = pl.ds(2 * half, 2)
        return self.w.at[(self.units(g, axis), *index, self.core)]

    def copy(self, ref, sent, recv, device):
        return pltpu.make_async_remote_copy(
            src_ref=ref, dst_ref=ref, send_sem=sent, recv_sem=recv,
            device_id=device, device_id_type=MESH,
        )

    def wait_for(self, ref, sem):
        self.copy(ref, self.sent_sem.at[0, 0, 0], sem, self.device(self.at, 1 - self.core)).wait_recv()

    def to_mate(self, g, axis, step):
        self.copy(
            self.slab(g, axis, step), self.sent_sem.at[g, axis, 3], self.mate_sem.at[g, axis],
            self.device(self.at, 1 - self.core),
        ).start()

    def greet(self):
        barrier = pltpu.get_barrier_semaphore()
        for axis in range(3):
            peer = self.plane(axis)

            @pl.loop(1, K * K)
            def _(i):
                pl.semaphore_signal(
                    barrier, inc=1, device_id=self.device(peer(i)), device_id_type=MESH
                )

        pl.semaphore_signal(
            barrier, inc=1, device_id=self.device(self.at, 1 - self.core), device_id_type=MESH
        )
        pl.semaphore_wait(barrier, 3 * (K * K - 1) + 1)

    def begin(self, g):
        for axis in range(3):
            peer = self.plane(axis)

            @pl.loop(1, K * K)
            def _(i):
                self.copy(
                    self.own(g, axis), self.sent_sem.at[g, axis, 0], self.near_sem.at[g, axis],
                    self.device(peer(i)),
                ).start()

    def second(self, g):
        for axis in range(3):
            k = ROUNDS[g][1]
            self.wait_for(self.blank.at[pl.ds(0, (K * K - 1) * k)], self.near_sem.at[g, axis])
            for side, step in enumerate((1, 3)):
                self.copy(
                    self.slab(g, axis, 0), self.sent_sem.at[g, axis, 1],
                    self.side_sem.at[g, axis, side], self.device(self.along(axis, step)),
                ).start()
        for axis in range(3):
            self.to_mate(g, axis, 0)

    def third(self, g):
        for axis in range(3):
            for side, step in enumerate((1, 3)):
                self.wait_for(self.slab(g, axis, 4 - step), self.side_sem.at[g, axis, side])
                self.copy(
                    self.slab(g, axis, 4 - step, side), self.sent_sem.at[g, axis, 2],
                    self.far_sem.at[g, axis, side], self.device(self.along(axis, step)),
                ).start()
            self.to_mate(g, axis, 1)
            self.to_mate(g, axis, 3)

    def fourth(self, g):
        for axis in range(3):
            for side in range(2):
                self.wait_for(self.slab(g, axis, 2, side), self.far_sem.at[g, axis, side])
            self.to_mate(g, axis, 2)

    def ready(self, g, axes=(0, 1, 2)):
        for axis in axes:
            self.wait_for(
                self.w.at[(self.units(g, axis), slice(None), slice(None), slice(None), self.core)],
                self.mate_sem.at[g, axis],
            )

    def close(self):
        for g in range(len(ROUNDS)):
            k = ROUNDS[g][1]
            for axis in range(3):
                units = self.units(g, axis)
                everything = (slice(None),) * 3
                for phase, ref in enumerate((
                    self.blank.at[pl.ds(0, (K * K - 1) * k)],
                    self.w.at[(units, pl.ds(0, 2), slice(None), slice(None), self.core)],
                    self.w.at[(units, pl.ds(0, 1), slice(None), slice(None), self.core)],
                    self.w.at[(units, *everything, self.core)],
                )):
                    self.copy(
                        ref, self.sent_sem.at[g, axis, phase], self.near_sem.at[g, axis],
                        self.device(self.at, 1 - self.core),
                    ).wait_send()


def push(me, d, src, dst, send_sem, recv_sem):
    return pltpu.make_async_remote_copy(
        src_ref=src,
        dst_ref=dst,
        send_sem=send_sem,
        recv_sem=recv_sem,
        device_id={"seq": lax.rem(me + d, N)},
        device_id_type=MESH,
    )


def roll(a):
    return pltpu.roll(a.astype(F32), 64, 1).astype(BF)


KEY, VALUE, QUERY, OUT = 0, 1, 2, 3
LAYER_UNITS = ((4, 5, 6, 7), (8, 9, 10, 11))


def kernel(
    off_ref, ctx_any, lat_any, qg_any, kg_any, lg_any, cq_any, ck_any, cv_any, co_any, lq_any, lo_any,
    out_ref,
    ctx, lat, qg, kg, lg, w, blank, cn, ln, keys, vals, queries, bias, part, stat, got, gstat,
    acc, den, att, hid, norm, qkv, qk_out, v_out, qk_in, v_in, m_out, m_in, merged,
    load_sem, shard_sem, near_sem, side_sem, far_sem, mate_sem, sent_sem,
    send_sem, recv_sem, ssend_sem, srecv_sem, lsend_sem, lrecv_sem,
):
    me = lax.axis_index("seq")
    gather = Gather(w, blank, (near_sem, side_sem, far_sem, mate_sem, sent_sem))
    shards = [ck_any, cv_any, cq_any, co_any]
    for l in range(2):
        shards += [lq_any.at[l, :, pl.ds(D * t, D)] for t in range(3)] + [lo_any.at[l]]
    shards = [
        pltpu.make_async_copy(s, w.at[(u, *gather.at, gather.core)], shard_sem.at[u])
        for u, s in enumerate(shards)
    ]
    loads = [
        pltpu.make_async_copy(a, b, load_sem.at[i])
        for i, (a, b) in enumerate((
            (kg_any, kg), (ctx_any.at[0], ctx), (qg_any, qg), (lat_any.at[0], lat), (lg_any, lg),
        ))
    ]
    for c in shards[:3] + loads + shards[3:]:
        c.start()
    gather.greet()
    for c in shards[:3]:
        c.wait()
    gather.begin(0)
    C = ctx.shape[0]
    M = lat.shape[0]
    R = M // N
    S = 128
    edge = me * C - off_ref[0]
    loads[0].wait()
    loads[1].wait()

    @pl.loop(0, C // S)
    def _(r):
        rows = pl.ds(pl.multiple_of(r * S, S), S)
        cn[rows] = normed_rows(ctx[rows], kg[...])

    stat[...] = jnp.zeros_like(stat)
    gather.second(0)
    for c in shards[3:]:
        c.wait()
    gather.begin(1)
    loads[2].wait()
    loads[3].wait()
    loads[4].wait()

    @pl.loop(0, M // S)
    def _(r):
        rows = pl.ds(pl.multiple_of(r * S, S), S)
        ln[rows] = normed_rows(lat[rows], qg[...])
        i = lax.broadcasted_iota(jnp.int32, (S, C), 0) + r * S
        j = lax.broadcasted_iota(jnp.int32, (S, C), 1)
        bias[rows] = jnp.where(j + edge <= i, 0.0, NEGATIVE)

    gather.third(0)
    gather.fourth(0)
    gather.second(1)
    gather.ready(0)

    def unit(u, cols):
        return w[u, :, :, :, :, :, cols].reshape(D, -1)

    @pl.loop(0, D // 256)
    def _(n):
        cols = pl.ds(pl.multiple_of(n * 256, 256), 256)
        k = dot(cn[...], unit(KEY, cols)).astype(BF)
        keys[2 * n] = k[:, :128]
        keys[2 * n + 1] = k[:, 128:]
        v = dot(cn[...], unit(VALUE, cols)).astype(BF)
        for t in range(2):
            vals[2 * n + t, :, 0:128] = v[:, 128 * t : 128 * t + 128]
            vals[2 * n + t, :, 128:256] = jnp.ones((C, 128), BF)

        @pl.loop(0, 2)
        def _(m):
            rows = pl.ds(pl.multiple_of(m * (M // 2), M // 2), M // 2)
            q = dot(ln[rows], unit(QUERY, cols)).astype(BF) * 0.125
            queries[2 * n, rows] = q[:, :128]
            queries[2 * n + 1, rows] = q[:, 128:]

    T = 128

    @pl.loop(0, H // 2)
    def _(p):
        @pl.loop(0, M // T)
        def _(r):
            rows = pl.ds(pl.multiple_of(r * T, T), T)
            q = queries[p, rows]
            low = lanes(T) < 64
            outs = []
            st = stat[rows]
            for t in range(2):
                qt = jnp.where(low if t == 0 else ~low, q, jnp.zeros_like(q))
                s = dot_t(qt, keys[p]) + bias[rows]
                top = jnp.max(s, axis=1, keepdims=True)
                e = jnp.exp(s - top).astype(BF)
                o = dot(e, vals[p])
                total = o[:, 128:256]
                outs.append(o[:, 0:128] / total)
                st = jnp.where(lanes(T) == 2 * p + t, top + jnp.log(total), st)
            part[p, rows] = jnp.where(low, outs[0], outs[1]).astype(BF)
            stat[rows] = st

        @pl.loop(1, N)
        def _(d):
            there = pl.ds(pl.multiple_of(lax.rem(me + d, N) * R, R), R)
            push(me, d, part.at[p, there], got.at[d - 1, p], send_sem, recv_sem.at[d - 1]).start()

        @pl.when(p == 1)
        def _():
            gather.third(1)
            gather.begin(2)

        @pl.when(p == 4)
        def _():
            gather.fourth(1)
            gather.second(2)

    @pl.loop(1, N)
    def _(d):
        there = pl.ds(pl.multiple_of(lax.rem(me + d, N) * R, R), R)
        push(me, d, stat.at[there], gstat.at[d - 1], ssend_sem, srecv_sem).start()

    gather.third(2)
    own = pl.ds(pl.multiple_of(me * R, R), R)
    push(me, 1, gstat, gstat, ssend_sem, srecv_sem).wait_recv()
    top = stat[own]
    for d in range(N - 1):
        top = jnp.maximum(top, gstat[d])
    spread = (
        lax.broadcasted_iota(jnp.int32, (128, D), 1) // 64
        == lax.broadcasted_iota(jnp.int32, (128, D), 0)
    ).astype(F32).astype(BF)
    weight = dot(jnp.exp(stat[own] - top).astype(BF), spread)
    den[...] = weight
    for p in range(H // 2):
        cols = slice(128 * p, 128 * p + 128)
        acc[:, cols] = weight[:, cols] * part[p, own].astype(F32)

    @pl.loop(0, N - 1)
    def _(d):
        push(me, 1, got.at[d], got.at[d], send_sem, recv_sem.at[d]).wait_recv()
        weight = dot(jnp.exp(gstat[d] - top).astype(BF), spread)
        den[...] += weight
        for p in range(H // 2):
            cols = slice(128 * p, 128 * p + 128)
            acc[:, cols] += weight[:, cols] * got[d, p].astype(F32)

    att[...] = (acc[...] / den[...]).astype(BF)
    gather.ready(1)
    hid[...] = lat[own]

    def add_update(rows_ref, u):
        @pl.loop(0, D // 256)
        def _(n):
            cols = pl.ds(pl.multiple_of(n * 256, 256), 256)
            update = dot(rows_ref[...], unit(u, cols))
            hid[:, cols] = (hid[:, cols].astype(F32) + update).astype(BF)

    add_update(att, OUT)
    low = lanes(R) < 64
    half = R // 2
    lo = lanes(half) < 64
    rest = pl.ds(0, N - 1)

    def exchange(l, t, src, dst, start):
        if start:
            @pl.loop(1, N)
            def _(d):
                to = lax.rem(me + d, N)
                push(me, d, src.at[to], dst.at[l, me], lsend_sem.at[l, t], lrecv_sem.at[l, t]).start()

            dst[l, me] = src[me]
        return push(me, 1, dst.at[l, rest], dst.at[l, rest], lsend_sem.at[l, t], lrecv_sem.at[l, t])

    for l in range(2):
        units = LAYER_UNITS[l]
        if l == 1:
            gather.ready(2)
        norm[...] = normed_rows(hid[...], lg[l : l + 1])
        for t in range(3):
            @pl.loop(0, D // 256)
            def _(n):
                cols = pl.ds(pl.multiple_of(n * 256, 256), 256)
                qkv[:, pl.ds(pl.multiple_of(D * t + n * 256, 256), 256)] = dot(
                    norm[...], unit(units[t], cols)
                ).astype(BF)

        if l == 1:
            exchange(0, 0, qk_out, qk_in, False).wait_send()
            exchange(0, 1, v_out, v_in, False).wait_send()
            exchange(0, 2, m_out, m_in, False).wait_send()
        for p in range(H // 2):
            q = qkv[:, 128 * p : 128 * p + 128] * 0.125
            k = qkv[:, D + 128 * p : D + 128 * p + 128]
            v = qkv[:, 2 * D + 128 * p : 2 * D + 128 * p + 128]
            qk_out[2 * p] = jnp.where(low, q, roll(k))
            qk_out[2 * p + 1] = jnp.where(low, roll(q), k)
            vr = roll(v)
            v_out[2 * p] = jnp.where(lo, v[:half], vr[half:])
            v_out[2 * p + 1] = jnp.where(lo, vr[:half], v[half:])
        exchange(l, 0, qk_out, qk_in, True)
        exchange(l, 1, v_out, v_in, True)
        if l == 0:
            gather.fourth(2)
        exchange(l, 0, qk_out, qk_in, False).wait_recv()
        exchange(l, 1, v_out, v_in, False).wait_recv()

        qk = qk_in[l].reshape(M, 128)
        kk = roll(qk)
        vp = v_in[l]
        vr = roll(vp.reshape(M // 2, 128)).reshape(N, half, 128)
        both = jnp.concatenate([vp, vr], axis=1).reshape(M, 128)
        vv = jnp.where(lanes(M) < 64, both, jnp.ones_like(both))
        for r in range(M // T):
            size = (r + 1) * T
            q = qk[r * T : size]
            q = jnp.where(lanes(T) < 64, q, jnp.zeros_like(q))
            s = dot_t(q, kk[:size])
            i = lax.broadcasted_iota(jnp.int32, (T, size), 0) + r * T
            j = lax.broadcasted_iota(jnp.int32, (T, size), 1)
            s = jnp.where(j <= i, s, NEGATIVE)
            top = jnp.max(s, axis=1, keepdims=True)
            e = jnp.exp(s - top).astype(BF)
            o = dot(e, vv[:size])
            mixed = o / pltpu.roll(o, 64, 1)
            other = pltpu.roll(mixed, 64, 1)
            for t in range(T // R):
                m_out[r * (T // R) + t] = jnp.where(
                    lo, mixed[t * R : t * R + half], other[t * R + half : t * R + R]
                ).astype(BF)

        exchange(l, 2, m_out, m_in, True)
        exchange(l, 2, m_out, m_in, False).wait_recv()
        for p in range(H // 2):
            a = m_in[l, 2 * p]
            b = m_in[l, 2 * p + 1]
            merged[0:half, 128 * p : 128 * p + 128] = jnp.where(lo, a, roll(b))
            merged[half:R, 128 * p : 128 * p + 128] = jnp.where(lo, roll(a), b)
        add_update(merged, units[3])

    out_ref[0] = hid[...]
    push(me, 1, got, got, send_sem, recv_sem.at[0]).wait_send()
    push(me, 1, gstat, gstat, ssend_sem, srecv_sem).wait_send()
    exchange(1, 0, qk_out, qk_in, False).wait_send()
    exchange(1, 1, v_out, v_in, False).wait_send()
    exchange(1, 2, m_out, m_in, False).wait_send()
    gather.close()


VM = pl.BlockSpec(memory_space=pltpu.VMEM)
SM = pl.BlockSpec(memory_space=pltpu.SMEM)
ANY = pl.BlockSpec(memory_space=pl.ANY)
DMA = pltpu.SemaphoreType.DMA


def per_device(
    context,
    latents,
    offsets,
    query_gain,
    key_gain,
    layer_gain,
    cross_query,
    cross_key,
    cross_value,
    cross_out,
    layer_qkv,
    layer_out,
):
    C, M = context.shape[1], latents.shape[1]
    R = M // N
    G = len(ROUNDS)
    most = max(k for _, k in ROUNDS)
    return pl.pallas_call(
        kernel,
        out_shape=jax.ShapeDtypeStruct((1, R, D), BF),
        in_specs=[SM] + [ANY] * 11,
        out_specs=VM,
        scratch_shapes=[
            pltpu.VMEM((C, D), BF),
            pltpu.VMEM((M, D), BF),
            pltpu.VMEM((1, D), F32),
            pltpu.VMEM((1, D), F32),
            pltpu.VMEM((2, D), F32),
            pltpu.VMEM((12, K, K, K, 2, 8, D), BF),
            pltpu.VMEM(((K * K - 1) * most, 8, D), BF),
            pltpu.VMEM((C, D), BF),
            pltpu.VMEM((M, D), BF),
            pltpu.VMEM((H // 2, C, 128), BF),
            pltpu.VMEM((H // 2, C, 256), BF),
            pltpu.VMEM((H // 2, M, 128), BF),
            pltpu.VMEM((M, C), F32),
            pltpu.VMEM((H // 2, M, 128), BF),
            pltpu.VMEM((M, 128), F32),
            pltpu.VMEM((N - 1, H // 2, R, 128), BF),
            pltpu.VMEM((N - 1, R, 128), F32),
            pltpu.VMEM((R, D), F32),
            pltpu.VMEM((R, D), F32),
            pltpu.VMEM((R, D), BF),
            pltpu.VMEM((R, D), BF),
            pltpu.VMEM((R, D), BF),
            pltpu.VMEM((R, 3 * D), BF),
            pltpu.VMEM((H, R, 128), BF),
            pltpu.VMEM((H, R // 2, 128), BF),
            pltpu.VMEM((2, N, R, 128), BF),
            pltpu.VMEM((2, N, R // 2, 128), BF),
            pltpu.VMEM((N, R // 2, 128), BF),
            pltpu.VMEM((2, H, R // 2, 128), BF),
            pltpu.VMEM((R, D), BF),
            DMA((5,)),
            DMA((12,)),
            DMA((G, 3)),
            DMA((G, 3, 2)),
            DMA((G, 3, 2)),
            DMA((G, 3)),
            DMA((G, 3, 4)),
            DMA,
            DMA((N - 1,)),
            DMA,
            DMA,
            DMA((2, 3)),
            DMA((2, 3)),
        ],
        compiler_params=pltpu.CompilerParams(
            collective_id=0, has_side_effects=True, vmem_limit_bytes=60 << 20
        ),
        name="window",
    )(
        offsets, context, latents, query_gain[None], key_gain[None], layer_gain,
        cross_query, cross_key, cross_value, cross_out, layer_qkv, layer_out,
    )

def solution(mesh):
    return jax.shard_map(
        per_device,
        mesh=mesh,
        in_specs=(
            P("head", "seq", None),
            P("head", None, None),
            P("head"),
            P(),
            P(),
            P(),
            P(("seq", "head"), None),
            P(("seq", "head"), None),
            P(("seq", "head"), None),
            P(("seq", "head"), None),
            P(None, ("seq", "head"), None),
            P(None, ("seq", "head"), None),
        ),
        out_specs=P("head", "seq", None),
        check_vma=False,
    )
```

time: 261 us -> 147 us (0.56)
  waiting for transfers between devices: 132 us -> 0 us
  Pallas kernels: 103 us -> 145 us
  between operations: 13.8 us -> 0.66 us
  local copies, waits for them, and re-layouts: 8.12 us -> 1.57 us
  other arithmetic: 3.34 us -> 0 us
    all_gather x3 -> x0, waiting for transfers between devices: 132 us -> none  [gather(): lax.all_gather(jnp.concatenate(pieces, axis=1), ('seq', 'head'), axis=0,...]
    pallas_call x3 -> x1, Pallas kernels: 103 us -> 145 us  [per_device(): pl.pallas_call(kernel, out_shape=jax.ShapeDtypeStruct((1, R, D), BF), in_...]
    concatenate x3 -> x0, other arithmetic: 3.34 us -> none  [gather(): jnp.concatenate(pieces, axis=1)]
    unnamed x9 -> x1, local copies, waits for them, and re-layouts: 4.85 us -> 1.57 us
  transfers between devices with their start and end apart: 3 -> 0, of which waited for: 3 -> 0; matrix products, arithmetic and copies ran while one was open for 2% -> 0% of each run, Pallas kernels for 31% -> 0%
where the time goes in v1:
time: 147 us
  Pallas kernels  145 us (99%)
  local copies, waits for them, and re-layouts  1.57 us (1%)
    pallas_call x1, Pallas kernels, per_device(): pl.pallas_call(kernel, out_shape=jax.ShapeDtypeStruct((1, R, D), BF), in_...  145 us

profile of v1, /device:TPU:0, one launch (start us, length us, event | category | flops | bytes accessed | tf_op | source)
XLA Modules:
  0.0 147.0 jit_solution(5778616142220743178)
XLA Ops:
  0.7 144.8 %window.1 = bf16[1,64,1024]{2,1,0:T(8,128)(2,1)} custom-call(s32[1]{0:T(128)S(6)} %copy.14.off_ref, bf16[1,512,1024]{2,1,0:T(8,128)(2,1)} %ctx_any.1, bf16[1,1024,1024]{2,1,0:T(8,128)(2,1)} %lat_any.1, f32[1,1024]{1,0:T(1,128)} %bitcast.2, f32[1,1024]{1,0:T(1,128)} %bitcast.3, f32[2,1024]{1,0:T(2,128)} %lg_any.1, bf16[8,1024]{1,0:T(8,128)(2,1)} %cq_any.1, ...), custom_call_target="tpu_custom_call" | custom-call | tf_op jit(solution)/shard_map/window/pallas_call | solution.py:480
  145.4 1.6 %copy.15 = bf16[1,64,1024]{2,1,0:T(8,128)(2,1)} copy(bf16[1,64,1024]{2,1,0:T(8,128)(2,1)} %window.1) | data formatting | bytes 262144

commit v2 on v1

v2 whole, which is shorter than its diff:
```python
import functools

import jax
import jax.numpy as jnp
from jax import lax
from jax.experimental import pallas as pl
from jax.experimental.pallas import tpu as pltpu
from jax.sharding import PartitionSpec as P

H = 16
EPSILON = 1e-06
NEGATIVE = -1e30
BF = jnp.bfloat16
F32 = jnp.float32
MESH = pl.DeviceIdType.MESH
N = 16
D = 1024


def normed_rows(x, gain):
    x = x.astype(F32)
    scale = lax.rsqrt(jnp.mean(x * x, axis=-1, keepdims=True) + EPSILON)
    return (x * scale * gain).astype(BF)


def dot(a, b):
    return jnp.dot(a, b, preferred_element_type=F32)


def dot_t(a, b):
    return lax.dot_general(a, b, (((1,), (1,)), ((), ())), preferred_element_type=F32)


def lanes(rows, width=128):
    return lax.broadcasted_iota(jnp.int32, (rows, width), 1)


K = 4
X, Z, Y = 0, 1, 2
GROUPS = (
    (0, 1, X, Y, Z, 0),
    (1, 1, Y, X, Z, 0),
    (2, 1, Z, X, Y, 0),
    (3, 1, X, Y, Z, 0),
    (4, 1, Y, X, Z, 0),
    (5, 1, Z, X, Y, 0),
    (6, 2, Y, X, Z, 1),
    (8, 2, Y, Z, X, 1),
    (10, 2, X, Y, Z, 1),
    (12, 2, Z, Y, X, 1),
    (14, 2, Y, X, Z, 1),
    (16, 2, Y, Z, X, 1),
    (18, 2, X, Y, Z, 1),
    (20, 2, Z, Y, X, 1),
    (22, 2, Y, X, Z, 1),
)


class Gather:
    def __init__(self, w, blank, sems):
        self.w, self.blank = w, blank
        self.line_sem, self.near_sem, self.side_sem, self.far_sem, self.mate_sem, self.sent_sem = sems
        me, lane = lax.axis_index("seq"), lax.axis_index("head")
        self.me = me
        self.at = (me // K, lax.rem(me, K), lane // 2)
        self.core = lax.rem(lane, 2)

    def device(self, at, core=None):
        core = self.core if core is None else core
        return {"seq": at[0] * K + at[1], "head": at[2] * 2 + core}

    def mate(self):
        return self.device(self.at, 1 - self.core)

    def plane(self, axis):
        a, b = [i for i in range(3) if i != axis]
        flat = self.at[a] * K + self.at[b]

        def peer(i):
            j = lax.rem(flat + i, K * K)
            at = list(self.at)
            at[a], at[b] = j // K, lax.rem(j, K)
            return at

        return peer

    def along(self, axis, step):
        at = list(self.at)
        at[axis] = lax.rem(at[axis] + step, K)
        return at

    def units(self, g):
        return pl.ds(GROUPS[g][0], GROUPS[g][1])

    def own(self, g):
        return self.w.at[(self.units(g), *self.at, self.core)]

    def line(self, g):
        index = list(self.at)
        index[GROUPS[g][3]] = slice(None)
        return self.w.at[(self.units(g), *index, self.core)]

    def slab(self, g, step, half=None):
        axis = GROUPS[g][2]
        index = [slice(None)] * 3
        index[axis] = lax.rem(self.at[axis] + step, K)
        if half is not None:
            index[1 if axis == 0 else 0] = pl.ds(2 * half, 2)
        return self.w.at[(self.units(g), *index, self.core)]

    def copy(self, ref, sent, recv, device):
        return pltpu.make_async_remote_copy(
            src_ref=ref, dst_ref=ref, send_sem=sent, recv_sem=recv,
            device_id=device, device_id_type=MESH,
        )

    def wait_for(self, ref, sem):
        self.copy(ref, self.sent_sem.at[0, 0], sem, self.mate()).wait_recv()

    def blanks(self, g, n):
        return self.blank.at[pl.ds(0, n * GROUPS[g][1])]

    def to_mate(self, g, step):
        self.copy(
            self.slab(g, step), self.sent_sem.at[g, 3], self.mate_sem.at[g], self.mate()
        ).start()

    def greet(self):
        barrier = pltpu.get_barrier_semaphore()
        for axis in range(3):
            peer = self.plane(axis)

            @pl.loop(1, K * K)
            def _(i):
                pl.semaphore_signal(
                    barrier, inc=1, device_id=self.device(peer(i)), device_id_type=MESH
                )

        pl.semaphore_signal(barrier, inc=1, device_id=self.mate(), device_id_type=MESH)
        pl.semaphore_wait(barrier, 3 * (K * K - 1) + 1)

    def begin(self, *groups):
        for g in groups:
            _, k, axis, first, second, steps = GROUPS[g]
            if steps:
                for i in range(1, K):
                    self.copy(
                        self.own(g), self.sent_sem.at[g, 4], self.line_sem.at[g],
                        self.device(self.along(first, i)),
                    ).start()
            else:
                peer = self.plane(axis)

                @pl.loop(1, K * K)
                def _(i):
                    self.copy(
                        self.own(g), self.sent_sem.at[g, 0], self.near_sem.at[g],
                        self.device(peer(i)),
                    ).start()

    def first(self, *groups):
        for g in groups:
            self.wait_for(self.blanks(g, K - 1), self.line_sem.at[g])
            for i in range(1, K):
                self.copy(
                    self.line(g), self.sent_sem.at[g, 0], self.near_sem.at[g],
                    self.device(self.along(GROUPS[g][4], i)),
                ).start()

    def second(self, *groups):
        for g in groups:
            n = K * (K - 1) if GROUPS[g][5] else K * K - 1
            self.wait_for(self.blanks(g, n), self.near_sem.at[g])
            for side, step in enumerate((1, 3)):
                self.copy(
                    self.slab(g, 0), self.sent_sem.at[g, 1],
                    self.side_sem.at[g, side], self.device(self.along(GROUPS[g][2], step)),
                ).start()
        for g in groups:
            self.to_mate(g, 0)

    def third(self, *groups):
        for g in groups:
            for side, step in enumerate((1, 3)):
                self.wait_for(self.slab(g, 4 - step), self.side_sem.at[g, side])
                self.copy(
                    self.slab(g, 4 - step, side), self.sent_sem.at[g, 2],
                    self.far_sem.at[g, side], self.device(self.along(GROUPS[g][2], step)),
                ).start()
        for g in groups:
            self.to_mate(g, 1)
            self.to_mate(g, 3)

    def fourth(self, *groups):
        for g in groups:
            for side in range(2):
                self.wait_for(self.slab(g, 2, side), self.far_sem.at[g, side])
            self.to_mate(g, 2)

    def ready(self, *groups):
        for g in groups:
            self.wait_for(
                self.w.at[(self.units(g), slice(None), slice(None), slice(None), self.core)],
                self.mate_sem.at[g],
            )

    def close(self):
        full = slice(None)
        for g in range(len(GROUPS)):
            units = self.units(g)
            steps = GROUPS[g][5]
            ends = [
                (0, self.blanks(g, K * (K - 1) if steps else K * K - 1)),
                (1, self.w.at[(units, pl.ds(0, 2), full, full, self.core)]),
                (2, self.w.at[(units, pl.ds(0, 1), full, full, self.core)]),
                (3, self.w.at[(units, full, full, full, self.core)]),
            ]
            if steps:
                ends.append((4, self.blanks(g, K - 1)))
            for phase, ref in ends:
                self.copy(ref, self.sent_sem.at[g, phase], self.near_sem.at[g], self.mate()).wait_send()


def push(me, d, src, dst, send_sem, recv_sem):
    return pltpu.make_async_remote_copy(
        src_ref=src,
        dst_ref=dst,
        send_sem=send_sem,
        recv_sem=recv_sem,
        device_id={"seq": lax.rem(me + d, N)},
        device_id_type=MESH,
    )


def roll(a):
    return pltpu.roll(a.astype(F32), 64, 1).astype(BF)


def folded(block):
    out = block[0:8]
    for t in range(1, 8):
        out = out + pltpu.roll(block[8 * t : 8 * t + 8], 16 * t, 1)
    return out


def unfolded(small):
    return jnp.concatenate(
        [small] + [pltpu.roll(small, 128 - 16 * t, 1) for t in range(1, 8)], axis=0
    )


KEY, VALUE, QUERY = 0, 1, 2
OUT = 6
LAYER_UNITS = ((8, 10, 12, 14), (16, 18, 20, 22))
HALF = D // 2


def kernel(
    off_ref, ctx_any, lat_any, qg_any, kg_any, lg_any, cq_any, ck_any, cv_any, co_any, lq_any, lo_any,
    out_ref,
    ctx, lat, qg, kg, lg, w, blank, cn, ln, keys, vals, queries, bias, part, stat, fold,
    got1, gf1, mid, mf, got2, gf2,
    att, hid, norm, qk_out, v_out, qk_in, v_in, m_out, m_in, merged,
    load_sem, shard_sem, line_sem, near_sem, side_sem, far_sem, mate_sem, sent_sem,
    rs_send, rs_recv, lsend_sem, lrecv_sem,
):
    me = lax.axis_index("seq")
    gather = Gather(w, blank, (line_sem, near_sem, side_sem, far_sem, mate_sem, sent_sem))
    here = gather.at
    shards = [a.at[:, pl.ds(HALF * t, HALF)] for t in range(2) for a in (ck_any, cv_any, cq_any)]
    shards += [co_any.at[:, pl.ds(HALF * t, HALF)] for t in range(2)]
    for l in range(2):
        shards += [lq_any.at[l, :, pl.ds(HALF * t, HALF)] for t in range(6)]
        shards += [lo_any.at[l, :, pl.ds(HALF * t, HALF)] for t in range(2)]
    shards = [
        pltpu.make_async_copy(s, w.at[(u, *here, gather.core)], shard_sem.at[u])
        for u, s in enumerate(shards)
    ]
    loads = [
        pltpu.make_async_copy(a, b, load_sem.at[i])
        for i, (a, b) in enumerate((
            (kg_any, kg), (ctx_any.at[0], ctx), (qg_any, qg), (lat_any.at[0], lat), (lg_any, lg),
        ))
    ]
    for c in shards[:6] + loads + shards[6:]:
        c.start()
    gather.greet()
    for c in shards[:6]:
        c.wait()
    gather.begin(0, 1, 2)
    gather.begin(3, 4, 5)
    C = ctx.shape[0]
    M = lat.shape[0]
    R = M // N
    S = 128
    edge = me * C - off_ref[0]
    loads[0].wait()
    loads[1].wait()

    @pl.loop(0, C // S)
    def _(r):
        rows = pl.ds(pl.multiple_of(r * S, S), S)
        cn[rows] = normed_rows(ctx[rows], kg[...])

    stat[...] = jnp.zeros_like(stat)
    vals[:, :, 128:256] = jnp.ones((H // 2, C, 128), BF)
    for c in loads[2:] + shards[6:]:
        c.wait()
    gather.second(0, 1, 2)

    @pl.loop(0, M // S)
    def _(r):
        rows = pl.ds(pl.multiple_of(r * S, S), S)
        ln[rows] = normed_rows(lat[rows], qg[...])
        i = lax.broadcasted_iota(jnp.int32, (S, C), 0) + r * S
        j = lax.broadcasted_iota(jnp.int32, (S, C), 1)
        bias[rows] = jnp.where(j + edge <= i, 0.0, NEGATIVE)

    early, late = (6, 7, 8, 9), (10, 11, 12, 13, 14)
    gather.second(3, 4, 5)
    gather.third(0, 1, 2)
    gather.third(3, 4, 5)
    gather.begin(*early, *late)
    gather.fourth(0, 1, 2)
    gather.first(*early)
    gather.ready(0, 1, 2)

    def piece(u, n):
        cols = pl.ds(pl.multiple_of(n * 256, 256), 256)
        return w[u, :, :, :, :, :, cols].reshape(D, 256)

    def unit(u, n):
        return piece(u + n // 2, lax.rem(n, 2))

    def projections(side):
        @pl.loop(0, 2)
        def _(n):
            p = 4 * side + 2 * n
            k = dot(cn[...], piece(3 * side + KEY, n)).astype(BF)
            keys[p] = k[:, :128]
            keys[p + 1] = k[:, 128:]
            v = dot(cn[...], piece(3 * side + VALUE, n)).astype(BF)
            vals[p, :, 0:128] = v[:, :128]
            vals[p + 1, :, 0:128] = v[:, 128:]

            @pl.loop(0, 2)
            def _(m):
                rows = pl.ds(pl.multiple_of(m * (M // 2), M // 2), M // 2)
                q = dot(ln[rows], piece(3 * side + QUERY, n)).astype(BF) * 0.125
                queries[p, rows] = q[:, :128]
                queries[p + 1, rows] = q[:, 128:]

    projections(0)
    gather.fourth(3, 4, 5)
    gather.second(*early)
    gather.first(*late)
    gather.ready(3, 4, 5)
    projections(1)
    T = 128
    low_t = lanes(T) < 64

    @pl.loop(0, H // 2)
    def _(p):
        for r in range(M // T):
            rows = slice(r * T, r * T + T)
            q = queries[p, rows]
            outs = []
            st = stat[rows]
            for t in range(2):
                qt = jnp.where(low_t if t == 0 else ~low_t, q, jnp.zeros_like(q))
                s = dot_t(qt, keys[p]) + bias[rows]
                top = jnp.max(s, axis=1, keepdims=True)
                e = jnp.exp(s - top).astype(BF)
                o = dot(e, vals[p])
                total = o[:, 128:256]
                outs.append(o[:, 0:128] / total)
                st = jnp.where(lanes(T) == 2 * p + t, top + jnp.log(total), st)
            both = jnp.where(low_t, outs[0], outs[1]).astype(BF)
            part[p, r // 2, 2 * (r % 2)] = both[:R]
            part[p, r // 2, 2 * (r % 2) + 1] = both[R:]
            stat[rows] = st

        for a in range(2):
            @pl.when(lax.rem(p, 2) == a)
            def _():
                for i in range(1, K):
                    to = gather.along(a, i)
                    src = part.at[p, to[0]] if a == 0 else part.at[p, :, to[1]]
                    pltpu.make_async_remote_copy(
                        src_ref=src, dst_ref=got1.at[a, i - 1, p // 2],
                        send_sem=rs_send.at[0], recv_sem=rs_recv.at[0, a, i - 1],
                        device_id=gather.device(to), device_id_type=MESH,
                    ).start()

        @pl.when(p == 2)
        def _():
            gather.third(8, 9)

        @pl.when(p == 4)
        def _():
            gather.third(6, 7)

        @pl.when(p == 6)
        def _():
            gather.second(*late)

    for s in range(N):
        fold[s // K, s % K] = folded(stat[s * R : s * R + R])

    def hop(k, a, i, src, dst):
        return pltpu.make_async_remote_copy(
            src_ref=src, dst_ref=dst, send_sem=rs_send.at[k], recv_sem=rs_recv.at[k, a, i - 1],
            device_id=gather.device(gather.along(a, i)), device_id_type=MESH,
        )

    for a in range(2):
        for i in range(1, K):
            to = gather.along(a, i)
            src = fold.at[to[0]] if a == 0 else fold.at[:, to[1]]
            hop(1, a, i, src, gf1.at[a, i - 1]).start()
    gather.fourth(8, 9)

    def spread(a, q):
        lane = lax.broadcasted_iota(jnp.int32, (128, 128), 1)
        row = lax.broadcasted_iota(jnp.int32, (128, 128), 0)
        return (row == 4 * q + 2 * a + lane // 64).astype(F32).astype(BF)

    def weights_of(levels):
        top = functools.reduce(jnp.maximum, levels)
        ws = [jnp.exp(x - top).astype(BF).astype(F32) for x in levels]
        return ws, top + jnp.log(functools.reduce(jnp.add, ws))

    def blend(ws, parts, a, q):
        spreader = spread(a, q)
        total = None
        for wt, o in zip(ws, parts):
            wide = dot(wt, spreader)
            term = wide * o.astype(F32)
            total = (term, wide) if total is None else (total[0] + term, total[1] + wide)
        return total[0] / total[1]

    for a in range(2):
        for i in range(1, K):
            hop(0, a, i, got1.at[a, i - 1], got1.at[a, i - 1]).wait_recv()
            hop(1, a, i, gf1.at[a, i - 1], gf1.at[a, i - 1]).wait_recv()

        @pl.loop(0, K)
        def _(b):
            mine = fold[here[0], b] if a == 0 else fold[b, here[1]]
            ws, level = weights_of([mine] + [gf1[a, i, b] for i in range(3)])
            mf[a, b] = level
            ws = [unfolded(x).astype(BF) for x in ws]
            for q in range(4):
                own = part[2 * q + a, here[0], b] if a == 0 else part[2 * q + a, b, here[1]]
                mid[a, q, b] = blend(ws, [own] + [got1[a, i, q, b] for i in range(3)], a, q).astype(BF)

        for i in range(1, K):
            to = gather.along(1 - a, i)
            b = to[1 - a]
            hop(2, 1 - a, i, mid.at[a, :, b], got2.at[a, i - 1]).start()
            hop(3, 1 - a, i, mf.at[a, b], gf2.at[a, i - 1]).start()

    gather.fourth(6, 7)
    own_rows = pl.ds(pl.multiple_of(me * R, R), R)
    hid[...] = lat[own_rows]
    for a in range(2):
        for i in range(1, K):
            hop(2, 1 - a, i, got2.at[a, i - 1], got2.at[a, i - 1]).wait_recv()
            hop(3, 1 - a, i, gf2.at[a, i - 1], gf2.at[a, i - 1]).wait_recv()
        b = here[1 - a]
        ws, _ = weights_of([mf[a, b]] + [gf2[a, i] for i in range(3)])
        ws = [unfolded(x).astype(BF) for x in ws]
        for q in range(4):
            p = 2 * q + a
            att[:, 128 * p : 128 * p + 128] = blend(
                ws, [mid[a, q, b]] + [got2[a, i, q] for i in range(3)], a, q
            ).astype(BF)
    gather.ready(*early)

    def add_update(rows_ref, u):
        @pl.loop(0, D // 256)
        def _(n):
            cols = pl.ds(pl.multiple_of(n * 256, 256), 256)
            update = dot(rows_ref[...], unit(u, n))
            hid[:, cols] = (hid[:, cols].astype(F32) + update).astype(BF)

    add_update(att, OUT)
    low = lanes(R) < 64
    half = R // 2
    lo = lanes(half) < 64
    rest = pl.ds(0, N - 1)

    def give(l, t, to, src, dst):
        @pl.when(to != me)
        def _():
            pltpu.make_async_remote_copy(
                src_ref=src.at[to], dst_ref=dst.at[l, me],
                send_sem=lsend_sem.at[l, t], recv_sem=lrecv_sem.at[l, t],
                device_id={"seq": to}, device_id_type=MESH,
            ).start()

    def taken(l, t, dst):
        return push(me, 1, dst.at[l, rest], dst.at[l, rest], lsend_sem.at[l, t], lrecv_sem.at[l, t])

    for l in range(2):
        units = LAYER_UNITS[l]
        if l == 1:
            taken(0, 0, qk_in).wait_send()
            taken(0, 1, v_in).wait_send()
            taken(0, 2, m_in).wait_send()
        norm[...] = normed_rows(hid[...], lg[l : l + 1])

        @pl.loop(0, 4)
        def _(step):
            n = lax.rem(step + me // 4 + 1, 4)
            q4 = dot(norm[...], unit(units[0], n)).astype(BF) * 0.125
            k4 = dot(norm[...], unit(units[1], n)).astype(BF)
            v4 = dot(norm[...], unit(units[2], n)).astype(BF)
            for j in range(2):
                q, k, v = (a[:, 128 * j : 128 * j + 128] for a in (q4, k4, v4))
                to = 4 * n + 2 * j
                qk_out[to] = jnp.where(low, q, roll(k))
                qk_out[to + 1] = jnp.where(low, roll(q), k)
                vr = roll(v)
                v_out[to] = jnp.where(lo, v[:half], vr[half:])
                v_out[to + 1] = jnp.where(lo, vr[:half], v[half:])
            for j in range(4):
                give(l, 0, 4 * n + j, qk_out, qk_in)
                give(l, 1, 4 * n + j, v_out, v_in)

        qk_in[l, me] = qk_out[me]
        v_in[l, me] = v_out[me]
        if l == 0:
            gather.third(*late)
        taken(l, 0, qk_in).wait_recv()
        taken(l, 1, v_in).wait_recv()

        qk = qk_in[l].reshape(M, 128)
        kk = roll(qk)
        vp = v_in[l]
        vr = roll(vp.reshape(M // 2, 128)).reshape(N, half, 128)
        both = jnp.concatenate([vp, vr], axis=1).reshape(M, 128)
        vv = jnp.where(lanes(M) < 64, both, jnp.ones_like(both))
        for r in reversed(range(M // T)):
            size = (r + 1) * T
            q = qk[r * T : size]
            q = jnp.where(low_t, q, jnp.zeros_like(q))
            s = dot_t(q, kk[:size])
            i = lax.broadcasted_iota(jnp.int32, (T, size), 0) + r * T
            j = lax.broadcasted_iota(jnp.int32, (T, size), 1)
            s = jnp.where(j <= i, s, NEGATIVE)
            top = jnp.max(s, axis=1, keepdims=True)
            e = jnp.exp(s - top).astype(BF)
            o = dot(e, vv[:size])
            mixed = o / pltpu.roll(o, 64, 1)
            other = pltpu.roll(mixed, 64, 1)
            for t in range(T // R):
                to = r * (T // R) + t
                m_out[to] = jnp.where(
                    lo, mixed[t * R : t * R + half], other[t * R + half : t * R + R]
                ).astype(BF)
        for step in range(1, N):
            push(
                me, step, m_out.at[lax.rem(me + step, N)], m_in.at[l, me],
                lsend_sem.at[l, 2], lrecv_sem.at[l, 2],
            ).start()
        m_in[l, me] = m_out[me]
        if l == 0:
            gather.fourth(*late)
        taken(l, 2, m_in).wait_recv()
        for p in range(H // 2):
            a = m_in[l, 2 * p]
            b = m_in[l, 2 * p + 1]
            merged[0:half, 128 * p : 128 * p + 128] = jnp.where(lo, a, roll(b))
            merged[half:R, 128 * p : 128 * p + 128] = jnp.where(lo, roll(a), b)
        if l == 0:
            gather.ready(*late)
        add_update(merged, units[3])

    out_ref[0] = hid[...]
    hop(0, 0, 1, got1, got1).wait_send()
    hop(1, 0, 1, gf1, gf1).wait_send()
    hop(2, 0, 1, got2, got2).wait_send()
    hop(3, 0, 1, gf2, gf2).wait_send()
    taken(1, 0, qk_in).wait_send()
    taken(1, 1, v_in).wait_send()
    taken(1, 2, m_in).wait_send()
    gather.close()


VM = pl.BlockSpec(memory_space=pltpu.VMEM)
SM = pl.BlockSpec(memory_space=pltpu.SMEM)
ANY = pl.BlockSpec(memory_space=pl.ANY)
DMA = pltpu.SemaphoreType.DMA


def per_device(
    context,
    latents,
    offsets,
    query_gain,
    key_gain,
    layer_gain,
    cross_query,
    cross_key,
    cross_value,
    cross_out,
    layer_qkv,
    layer_out,
):
    C, M = context.shape[1], latents.shape[1]
    R = M // N
    G = len(GROUPS)
    most = max(g[1] for g in GROUPS)
    return pl.pallas_call(
        kernel,
        out_shape=jax.ShapeDtypeStruct((1, R, D), BF),
        in_specs=[SM] + [ANY] * 11,
        out_specs=VM,
        scratch_shapes=[
            pltpu.VMEM((C, D), BF),
            pltpu.VMEM((M, D), BF),
            pltpu.VMEM((1, D), F32),
            pltpu.VMEM((1, D), F32),
            pltpu.VMEM((2, D), F32),
            pltpu.VMEM((24, K, K, K, 2, 8, HALF), BF),
            pltpu.VMEM(((K * K - 1) * most, 8, HALF), BF),
            pltpu.VMEM((C, D), BF),
            pltpu.VMEM((M, D), BF),
            pltpu.VMEM((H // 2, C, 128), BF),
            pltpu.VMEM((H // 2, C, 256), BF),
            pltpu.VMEM((H // 2, M, 128), BF),
            pltpu.VMEM((M, C), F32),
            pltpu.VMEM((H // 2, K, K, R, 128), BF),
            pltpu.VMEM((M, 128), F32),
            pltpu.VMEM((K, K, 8, 128), F32),
            pltpu.VMEM((2, K - 1, 4, K, R, 128), BF),
            pltpu.VMEM((2, K - 1, K, 8, 128), F32),
            pltpu.VMEM((2, 4, K, R, 128), BF),
            pltpu.VMEM((2, K, 8, 128), F32),
            pltpu.VMEM((2, K - 1, 4, R, 128), BF),
            pltpu.VMEM((2, K - 1, 8, 128), F32),
            pltpu.VMEM((R, D), BF),
            pltpu.VMEM((R, D), BF),
            pltpu.VMEM((R, D), BF),
            pltpu.VMEM((H, R, 128), BF),
            pltpu.VMEM((H, R // 2, 128), BF),
            pltpu.VMEM((2, N, R, 128), BF),
            pltpu.VMEM((2, N, R // 2, 128), BF),
            pltpu.VMEM((N, R // 2, 128), BF),
            pltpu.VMEM((2, H, R // 2, 128), BF),
            pltpu.VMEM((R, D), BF),
            DMA((5,)),
            DMA((24,)),
            DMA((G,)),
            DMA((G,)),
            DMA((G, 2)),
            DMA((G, 2)),
            DMA((G,)),
            DMA((G, 5)),
            DMA((4,)),
            DMA((4, 2, 3)),
            DMA((2, 3)),
            DMA((2, 3)),
        ],
        compiler_params=pltpu.CompilerParams(
            collective_id=0, has_side_effects=True, vmem_limit_bytes=60 << 20
        ),
        name="window",
    )(
        offsets, context, latents, query_gain[None], key_gain[None], layer_gain,
        cross_query, cross_key, cross_value, cross_out, layer_qkv, layer_out,
    )

def solution(mesh):
    return jax.shard_map(
        per_device,
        mesh=mesh,
        in_specs=(
            P("head", "seq", None),
            P("head", None, None),
            P("head"),
            P(),
            P(),
            P(),
            P(("seq", "head"), None),
            P(("seq", "head"), None),
            P(("seq", "head"), None),
            P(("seq", "head"), None),
            P(None, ("seq", "head"), None),
            P(None, ("seq", "head"), None),
        ),
        out_specs=P("head", "seq", None),
        check_vma=False,
    )
```

time: 147 us -> 116 us (0.79)
  Pallas kernels: 145 us -> 113 us
    pallas_call x1, Pallas kernels: 145 us -> 113 us  [per_device(): pl.pallas_call(kernel, out_shape=jax.ShapeDtypeStruct((1, R, D), BF), in_...]
where the time goes in v2:
time: 116 us
  Pallas kernels  113 us (97%)
  local copies, waits for them, and re-layouts  1.57 us (1%)
    pallas_call x1, Pallas kernels, per_device(): pl.pallas_call(kernel, out_shape=jax.ShapeDtypeStruct((1, R, D), BF), in_...  113 us

profile of v2, /device:TPU:0, one launch (start us, length us, event | category | flops | bytes accessed | tf_op | source)
XLA Modules:
  0.0 115.5 jit_solution(9059873037914498652)
XLA Ops:
  0.7 113.3 %window.1 = bf16[1,64,1024]{2,1,0:T(8,128)(2,1)} custom-call(s32[1]{0:T(128)S(6)} %copy.14.off_ref, bf16[1,512,1024]{2,1,0:T(8,128)(2,1)} %ctx_any.1, bf16[1,1024,1024]{2,1,0:T(8,128)(2,1)} %lat_any.1, f32[1,1024]{1,0:T(1,128)} %bitcast.2, f32[1,1024]{1,0:T(1,128)} %bitcast.3, f32[2,1024]{1,0:T(2,128)} %lg_any.1, bf16[8,1024]{1,0:T(8,128)(2,1)} %cq_any.1, ...), custom_call_target="tpu_custom_call" | custom-call | tf_op jit(solution)/shard_map/window/pallas_call | solution.py:615
  114.0 1.6 %copy.15 = bf16[1,64,1024]{2,1,0:T(8,128)(2,1)} copy(bf16[1,64,1024]{2,1,0:T(8,128)(2,1)} %window.1) | data formatting | bytes 262144

commit v3 on v2

--- a/solution.py
+++ b/solution.py
@@ -289,6 +289,10 @@
         c.wait()
     gather.begin(0, 1, 2)
     gather.begin(3, 4, 5)
+    early, late = (6, 7, 8, 9), (10, 11, 12, 13, 14)
+    for c in shards[6:]:
+        c.wait()
+    gather.begin(*early)
     C = ctx.shape[0]
     M = lat.shape[0]
     R = M // N
@@ -304,7 +308,7 @@
 
     stat[...] = jnp.zeros_like(stat)
     vals[:, :, 128:256] = jnp.ones((H // 2, C, 128), BF)
-    for c in loads[2:] + shards[6:]:
+    for c in loads[2:]:
         c.wait()
     gather.second(0, 1, 2)
 
@@ -316,11 +320,10 @@
         j = lax.broadcasted_iota(jnp.int32, (S, C), 1)
         bias[rows] = jnp.where(j + edge <= i, 0.0, NEGATIVE)
 
-    early, late = (6, 7, 8, 9), (10, 11, 12, 13, 14)
     gather.second(3, 4, 5)
     gather.third(0, 1, 2)
     gather.third(3, 4, 5)
-    gather.begin(*early, *late)
+    gather.begin(*late)
     gather.fourth(0, 1, 2)
     gather.first(*early)
     gather.ready(0, 1, 2)
@@ -352,10 +355,12 @@
 
     projections(0)
     gather.fourth(3, 4, 5)
-    gather.second(*early)
-    gather.first(*late)
+    gather.second(6, 7)
+    gather.first(10, 11)
     gather.ready(3, 4, 5)
     projections(1)
+    gather.second(8, 9)
+    gather.first(12, 13, 14)
     T = 128
     low_t = lanes(T) < 64
 
@@ -392,17 +397,21 @@
                         device_id=gather.device(to), device_id_type=MESH,
                     ).start()
 
+        @pl.when(p == 1)
+        def _():
+            gather.third(6)
+
         @pl.when(p == 2)
         def _():
+            gather.second(10, 11)
+
+        @pl.when(p == 3)
+        def _():
+            gather.third(7)
+
+        @pl.when(p == 5)
+        def _():
             gather.third(8, 9)
-
-        @pl.when(p == 4)
-        def _():
-            gather.third(6, 7)
-
-        @pl.when(p == 6)
-        def _():
-            gather.second(*late)
 
     for s in range(N):
         fold[s // K, s % K] = folded(stat[s * R : s * R + R])
@@ -418,7 +427,6 @@
             to = gather.along(a, i)
             src = fold.at[to[0]] if a == 0 else fold.at[:, to[1]]
             hop(1, a, i, src, gf1.at[a, i - 1]).start()
-    gather.fourth(8, 9)
 
     def spread(a, q):
         lane = lax.broadcasted_iota(jnp.int32, (128, 128), 1)
@@ -460,7 +468,9 @@
             hop(2, 1 - a, i, mid.at[a, :, b], got2.at[a, i - 1]).start()
             hop(3, 1 - a, i, mf.at[a, b], gf2.at[a, i - 1]).start()
 
-    gather.fourth(6, 7)
+    gather.fourth(*early)
+    gather.second(12, 13, 14)
+    gather.third(10, 11)
     own_rows = pl.ds(pl.multiple_of(me * R, R), R)
     hid[...] = lat[own_rows]
     for a in range(2):
@@ -505,6 +515,7 @@
     for l in range(2):
         units = LAYER_UNITS[l]
         if l == 1:
+            gather.ready(11, 12, 13)
             taken(0, 0, qk_in).wait_send()
             taken(0, 1, v_in).wait_send()
             taken(0, 2, m_in).wait_send()
@@ -531,7 +542,10 @@
         qk_in[l, me] = qk_out[me]
         v_in[l, me] = v_out[me]
         if l == 0:
-            gather.third(*late)
+            gather.third(12, 13)
+            gather.fourth(10, 11)
+        else:
+            gather.fourth(14)
         taken(l, 0, qk_in).wait_recv()
         taken(l, 1, v_in).wait_recv()
 
@@ -566,15 +580,15 @@
             ).start()
         m_in[l, me] = m_out[me]
         if l == 0:
-            gather.fourth(*late)
+            gather.third(14)
+            gather.fourth(12, 13)
         taken(l, 2, m_in).wait_recv()
         for p in range(H // 2):
             a = m_in[l, 2 * p]
             b = m_in[l, 2 * p + 1]
             merged[0:half, 128 * p : 128 * p + 128] = jnp.where(lo, a, roll(b))
             merged[half:R, 128 * p : 128 * p + 128] = jnp.where(lo, roll(a), b)
-        if l == 0:
-            gather.ready(*late)
+        gather.ready(10 if l == 0 else 14)
         add_update(merged, units[3])
 
     out_ref[0] = hid[...]

time: 116 us -> 111 us (0.957)
  Pallas kernels: 113 us -> 108 us
    pallas_call x1, Pallas kernels: 113 us -> 108 us  [per_device(): pl.pallas_call(kernel, out_shape=jax.ShapeDtypeStruct((1, R, D), BF), in_...]
where the time goes in v3:
time: 111 us
  Pallas kernels  108 us (97%)
  local copies, waits for them, and re-layouts  1.57 us (1%)
    pallas_call x1, Pallas kernels, per_device(): pl.pallas_call(kernel, out_shape=jax.ShapeDtypeStruct((1, R, D), BF), in_...  108 us

profile of v3, /device:TPU:0, one launch (start us, length us, event | category | flops | bytes accessed | tf_op | source)
XLA Modules:
  0.0 110.7 jit_solution(14352323269868607420)
XLA Ops:
  0.7 108.4 %window.1 = bf16[1,64,1024]{2,1,0:T(8,128)(2,1)} custom-call(s32[1]{0:T(128)S(6)} %copy.14.off_ref, bf16[1,512,1024]{2,1,0:T(8,128)(2,1)} %ctx_any.1, bf16[1,1024,1024]{2,1,0:T(8,128)(2,1)} %lat_any.1, f32[1,1024]{1,0:T(1,128)} %bitcast.2, f32[1,1024]{1,0:T(1,128)} %bitcast.3, f32[2,1024]{1,0:T(2,128)} %lg_any.1, bf16[8,1024]{1,0:T(8,128)(2,1)} %cq_any.1, ...), custom_call_target="tpu_custom_call" | custom-call | tf_op jit(solution)/shard_map/window/pallas_call | solution.py:629
  109.1 1.6 %copy.15 = bf16[1,64,1024]{2,1,0:T(8,128)(2,1)} copy(bf16[1,64,1024]{2,1,0:T(8,128)(2,1)} %window.1) | data formatting | bytes 262144

commit v4 on v3

--- a/solution.py
+++ b/solution.py
@@ -346,7 +346,7 @@
             vals[p, :, 0:128] = v[:, :128]
             vals[p + 1, :, 0:128] = v[:, 128:]
 
-            @pl.loop(0, 2)
+            @pl.loop(0, 2, unroll=2)
             def _(m):
                 rows = pl.ds(pl.multiple_of(m * (M // 2), M // 2), M // 2)
                 q = dot(ln[rows], piece(3 * side + QUERY, n)).astype(BF) * 0.125
@@ -452,7 +452,7 @@
             hop(0, a, i, got1.at[a, i - 1], got1.at[a, i - 1]).wait_recv()
             hop(1, a, i, gf1.at[a, i - 1], gf1.at[a, i - 1]).wait_recv()
 
-        @pl.loop(0, K)
+        @pl.loop(0, K, unroll=K)
         def _(b):
             mine = fold[here[0], b] if a == 0 else fold[b, here[1]]
             ws, level = weights_of([mine] + [gf1[a, i, b] for i in range(3)])
@@ -485,16 +485,17 @@
             att[:, 128 * p : 128 * p + 128] = blend(
                 ws, [mid[a, q, b]] + [got2[a, i, q] for i in range(3)], a, q
             ).astype(BF)
-    gather.ready(*early)
+    gather.ready(6)
 
     def add_update(rows_ref, u):
-        @pl.loop(0, D // 256)
+        @pl.loop(0, D // 256, unroll=D // 256)
         def _(n):
             cols = pl.ds(pl.multiple_of(n * 256, 256), 256)
             update = dot(rows_ref[...], unit(u, n))
             hid[:, cols] = (hid[:, cols].astype(F32) + update).astype(BF)
 
     add_update(att, OUT)
+    gather.ready(7, 8, 9)
     low = lanes(R) < 64
     half = R // 2
     lo = lanes(half) < 64

time: 111 us -> 110 us (level)
  no operation moved by 1% of the time
where the time goes in v4:
time: 110 us
  Pallas kernels  107 us (97%)
  local copies, waits for them, and re-layouts  1.57 us (1%)
    pallas_call x1, Pallas kernels, per_device(): pl.pallas_call(kernel, out_shape=jax.ShapeDtypeStruct((1, R, D), BF), in_...  107 us

profile of v4, /device:TPU:0, one launch (start us, length us, event | category | flops | bytes accessed | tf_op | source)
XLA Modules:
  0.0 109.6 jit_solution(10478113376236702342)
XLA Ops:
  0.7 107.3 %window.1 = bf16[1,64,1024]{2,1,0:T(8,128)(2,1)} custom-call(s32[1]{0:T(128)S(6)} %copy.14.off_ref, bf16[1,512,1024]{2,1,0:T(8,128)(2,1)} %ctx_any.1, bf16[1,1024,1024]{2,1,0:T(8,128)(2,1)} %lat_any.1, f32[1,1024]{1,0:T(1,128)} %bitcast.2, f32[1,1024]{1,0:T(1,128)} %bitcast.3, f32[2,1024]{1,0:T(2,128)} %lg_any.1, bf16[8,1024]{1,0:T(8,128)(2,1)} %cq_any.1, ...), custom_call_target="tpu_custom_call" | custom-call | tf_op jit(solution)/shard_map/window/pallas_call | solution.py:630
  108.0 1.6 %copy.15 = bf16[1,64,1024]{2,1,0:T(8,128)(2,1)} copy(bf16[1,64,1024]{2,1,0:T(8,128)(2,1)} %window.1) | data formatting | bytes 262144

commit v5 on v4

--- a/solution.py
+++ b/solution.py
@@ -501,14 +501,18 @@
     lo = lanes(half) < 64
     rest = pl.ds(0, N - 1)
 
-    def give(l, t, to, src, dst):
-        @pl.when(to != me)
-        def _():
+    def give(l, t, to, src, dst, mine):
+        def start():
             pltpu.make_async_remote_copy(
                 src_ref=src.at[to], dst_ref=dst.at[l, me],
                 send_sem=lsend_sem.at[l, t], recv_sem=lrecv_sem.at[l, t],
                 device_id={"seq": to}, device_id_type=MESH,
             ).start()
+
+        if mine:
+            pl.when(to != me)(start)
+        else:
+            start()
 
     def taken(l, t, dst):
         return push(me, 1, dst.at[l, rest], dst.at[l, rest], lsend_sem.at[l, t], lrecv_sem.at[l, t])
@@ -522,8 +526,7 @@
             taken(0, 2, m_in).wait_send()
         norm[...] = normed_rows(hid[...], lg[l : l + 1])
 
-        @pl.loop(0, 4)
-        def _(step):
+        for step in range(4):
             n = lax.rem(step + me // 4 + 1, 4)
             q4 = dot(norm[...], unit(units[0], n)).astype(BF) * 0.125
             k4 = dot(norm[...], unit(units[1], n)).astype(BF)
@@ -537,8 +540,8 @@
                 v_out[to] = jnp.where(lo, v[:half], vr[half:])
                 v_out[to + 1] = jnp.where(lo, vr[:half], v[half:])
             for j in range(4):
-                give(l, 0, 4 * n + j, qk_out, qk_in)
-                give(l, 1, 4 * n + j, v_out, v_in)
+                give(l, 0, 4 * n + j, qk_out, qk_in, step == 3)
+                give(l, 1, 4 * n + j, v_out, v_in, step == 3)
 
         qk_in[l, me] = qk_out[me]
         v_in[l, me] = v_out[me]

time: 110 us -> 110 us (level)
  no operation moved by 1% of the time
where the time goes in v5:
time: 110 us
  Pallas kernels  107 us (97%)
  local copies, waits for them, and re-layouts  1.57 us (1%)
    pallas_call x1, Pallas kernels, per_device(): pl.pallas_call(kernel, out_shape=jax.ShapeDtypeStruct((1, R, D), BF), in_...  107 us

profile of v5, /device:TPU:0, one launch (start us, length us, event | category | flops | bytes accessed | tf_op | source)
XLA Modules:
  0.0 109.6 jit_solution(9049973960941340354)
XLA Ops:
  0.7 107.3 %window.1 = bf16[1,64,1024]{2,1,0:T(8,128)(2,1)} custom-call(s32[1]{0:T(128)S(6)} %copy.14.off_ref, bf16[1,512,1024]{2,1,0:T(8,128)(2,1)} %ctx_any.1, bf16[1,1024,1024]{2,1,0:T(8,128)(2,1)} %lat_any.1, f32[1,1024]{1,0:T(1,128)} %bitcast.2, f32[1,1024]{1,0:T(1,128)} %bitcast.3, f32[2,1024]{1,0:T(2,128)} %lg_any.1, bf16[8,1024]{1,0:T(8,128)(2,1)} %cq_any.1, ...), custom_call_target="tpu_custom_call" | custom-call | tf_op jit(solution)/shard_map/window/pallas_call | solution.py:633
  108.0 1.6 %copy.15 = bf16[1,64,1024]{2,1,0:T(8,128)(2,1)} copy(bf16[1,64,1024]{2,1,0:T(8,128)(2,1)} %window.1) | data formatting | bytes 262144
